TPU v7x, 32 devices: a whole 2x2x4 slice. The times are simulated.
32 devices in a mesh: rows: 4 (over y, x), feat: 8 (over z, core).
Axes of the slice: x: 2, y: 2, z: 4, core: 2. Of those that a mesh axis runs over, the one named last changes fastest.
Arguments:
- bins: int32 [256, 32768], P(None, ('rows', 'feat')), may hold values from 0 to 255
- leaf: int32 [32768], P(('rows', 'feat')), may hold values from 0 to 1
- grad: bfloat16 [32, 32768], P(None, ('rows', 'feat')), may hold values from -15.55 to 15.55
- hess: bfloat16 [32, 32768], P(None, ('rows', 'feat')), may hold values from 0.049804688 to 1
Outputs:
- gains: float32 [256, 2, 256], P(('rows', 'feat'))
- best: float32 [2], replicated
All inputs are finite; a program needn't handle non-finite values.
Results may differ from a plain program's by a relative error of at most 0.0003.
Values may be sent and summed in bfloat16 or wider, within the bound.
A program may use at most 128 MiB of HBM per device.

v0:
```python
import math
import jax
import jax.numpy as jnp
from jax import lax
from jax.sharding import PartitionSpec as P

F = 256
B = 256
LEAVES = 2


def leaf_weighted(both, leaf_row, leaves):
    nodes = jnp.arange(leaves, dtype=jnp.float32)[:, None]
    hot = (leaf_row.astype(jnp.float32) == nodes).astype(jnp.bfloat16)
    return (hot[:, None, :] * both[None, :, :]).reshape(leaves * both.shape[0], both.shape[1])


def bin_counts(codes, weighted, bin_total):
    levels = jnp.arange(bin_total, dtype=jnp.int32)
    onehot = (codes[:, :, None] == levels).astype(jnp.bfloat16)
    return jnp.einsum("frb,cr->fbc", onehot, weighted, preferred_element_type=jnp.float32)


def split_gains(hist, totals, outputs):
    count = hist.shape[0]
    cum = jnp.cumsum(hist, axis=1).reshape(count, B, LEAVES, 2, outputs)
    tot = totals.reshape(LEAVES, 2, outputs)
    left_grad = cum[:, :, :, 0, :]
    left_hess = cum[:, :, :, 1, :]
    all_grad = tot[:, 0, :]
    all_hess = tot[:, 1, :]
    right_grad = all_grad - left_grad
    right_hess = all_hess - left_hess
    score = (
        left_grad * left_grad / (left_hess + 1.0)
        + right_grad * right_grad / (right_hess + 1.0)
        - all_grad * all_grad / (all_hess + 1.0)
    )
    gains = 0.5 / outputs * jnp.sum(score, axis=-1)
    return jnp.transpose(gains, (0, 2, 1))


def shards(bins, leaf, grad, hess):
    outputs = grad.shape[0]
    shard = bins.shape[1]
    devices = lax.axis_size("rows") * lax.axis_size("feat")
    owned = F // devices
    both = jnp.concatenate([grad, hess], axis=0)
    leaf_row = leaf[None, :]
    weighted = leaf_weighted(both, leaf_row, LEAVES)
    columns = weighted.shape[0]
    codes_mine = lax.all_to_all(bins, ("rows", "feat"), split_axis=0, concat_axis=1, tiled=True)
    initial = jnp.zeros((owned, B, columns), jnp.float32)
    both_piece = lax.all_gather(both, ("rows", "feat"), axis=1, tiled=True)
    leaf_piece = lax.all_gather(leaf_row.astype(jnp.bfloat16), ("rows", "feat"), axis=1, tiled=True)
    length = both_piece.shape[1]
    width = math.gcd(length, 8 * shard)

    def step(index, total):
        offset = index * width
        part_codes = lax.dynamic_slice_in_dim(codes_mine, offset, width, 1)
        part_both = lax.dynamic_slice_in_dim(both_piece, offset, width, 1)
        part_leaf = lax.dynamic_slice_in_dim(leaf_piece, offset, width, 1)
        return total + bin_counts(part_codes, leaf_weighted(part_both, part_leaf, LEAVES), B)

    hist = lax.fori_loop(0, length // width, step, initial)
    totals = lax.psum(jnp.sum(weighted, axis=1, dtype=jnp.float32), ("rows", "feat"))
    gains = split_gains(hist, totals, outputs)
    best = lax.pmax(jnp.max(gains, axis=(0, 2)), ("rows", "feat"))
    return (gains, best)


def solution(mesh):
    return jax.shard_map(
        shards,
        mesh=mesh,
        in_specs=(
            P(None, ("rows", "feat")),
            P(("rows", "feat")),
            P(None, ("rows", "feat")),
            P(None, ("rows", "feat")),
        ),
        out_specs=(P(("rows", "feat"), None, None), P()),
        check_vma=False,
    )
```

profile of v0, /device:TPU:0, one launch (start us, length us, event | category | flops | bytes accessed | tf_op | source)
XLA Modules:
  0.0 226.1 jit_solution(3870619815995787336)
XLA Ops:
  7.2 0.0 copy-start.2
  7.2 0.0 all-gather.3.cloned.1.call-start
  7.2 0.8 constant_dynamic-update-slice_fusion.1
  8.1 0.8 constant_dynamic-update-slice_fusion
  8.9 0.0 copy-start
  8.9 0.6 copy-done
  9.5 0.0 all-gather.3.cloned.1.call-update
  9.6 0.0 copy-start.1
  9.6 7.3 %all-to-all-start = ((s32[32,8,1024]{2,1,0:T(8,128)}), s32[32,8,1024]{2,1,0:T(8,128)S(1)}, u32[]{:S(2)}, u32[]{:S(2)}) async-start(s32[32,8,1024]{2,1,0:T(8,128)} %bitcast.44), calls=%async_computation | async-start | bytes 2097152 | tf_op jit(solution)/shard_map/all_to_all | solution.py:52
  16.9 0.0 copy-done.2
  17.0 0.0 copy-done.1
  17.0 0.1 convert_reduce_fusion
  17.1 0.1 reshape.98
  17.2 60.4 %all-gather = bf16[32768]{0:T(1024)(128)(2,1)S(1)} all-gather(bf16[1024]{0:T(1024)(128)(2,1)S(1)} %get-tuple-element.128), channel_id=2, replica_groups=mesh['rows'=4,'feat'=8] {'rows','feat'}, dimensions={0}, use_global_device_ids=true | all-gather | bytes 67584 | tf_op jit(solution)/shard_map/all_gather | solution.py:55
  77.6 0.1 reshape.101
  77.6 37.5 %psum.7 = f32[2,2,32]{2,1,0:T(2,128)S(1)} all-reduce(f32[2,2,32]{2,1,0:T(2,128)S(1)} %reshape.98), channel_id=1, replica_groups=mesh['rows'=4,'feat'=8] {'rows','feat'}, use_global_device_ids=true, to_apply=%region_5.6 | all-reduce | flops 128 | bytes 1024 | tf_op jit(solution)/shard_map/psum | solution.py:67
  115.2 0.0 all-to-all-done
  115.2 0.0 all-gather.3.cloned.1.call-done
  115.2 58.8 %while.14 = (s32[]{:T(128)}, f32[8,256,128]{2,1,0:T(8,128)}, s32[8,32768]{1,0:T(8,128)S(1)}, bf16[1,32768]{1,0:T(2,128)(2,1)S(1)}, bf16[64,32768]{1,0:T(8,128)(2...) while((s32[]{:T(128)}, f32[8,256,128]{2,1,0:T(8,128)}, s32[8,32768]{1,0:T(8,128)S(1)}, ...), condition=%wide.region_1.0_spmd.clone, body=%wide.region_0.0_spmd.clone.sunk | while | flops 4313358336 | bytes 10371233 | solution.py:66
  115.2 1.3 constant_dynamic-slice_fusion.4
  116.6 0.2 broadcast_multiply_fusion.2
  116.8 12.3 %fusion.12 = f32[8,256,128]{2,1,0:T(8,128)} fusion(bf16[128,8192,1]{1,0,2:T(8,128)(2,1)S(1)} %bitcast.39, s32[8,8192]{1,0:T(8,128)S(1)} %constant_dynamic-slice_fusion.5, f32[8,256,128]{2,1,0:T(8,128)} %get-tuple-element.172, pred[]{:T(512)S(6)} %compare.3), kind=kOutput, calls=%fused_computation.3.clone.1 | convolution fusion | flops 4312268800 | bytes 4456449 | tf_op jit(solution)/shard_map/while/body/eval_jaxpr/frb,cr->fbc/dot_general | solution.py:21
  129.2 1.3 constant_dynamic-slice_fusion.4
  130.6 0.2 broadcast_multiply_fusion.2
  130.8 13.3 %fusion.12 = f32[8,256,128]{2,1,0:T(8,128)} fusion(bf16[128,8192,1]{1,0,2:T(8,128)(2,1)S(1)} %bitcast.39, s32[8,8192]{1,0:T(8,128)S(1)} %constant_dynamic-slice_fusion.5, f32[8,256,128]{2,1,0:T(8,128)} %get-tuple-element.172, pred[]{:T(512)S(6)} %compare.3), kind=kOutput, calls=%fused_computation.3.clone.1 | convolution fusion | flops 4312268800 | bytes 4456449 | tf_op jit(solution)/shard_map/while/body/eval_jaxpr/frb,cr->fbc/dot_general | solution.py:21
  144.1 1.3 constant_dynamic-slice_fusion.4
  145.5 0.2 broadcast_multiply_fusion.2
  145.7 13.4 %fusion.12 = f32[8,256,128]{2,1,0:T(8,128)} fusion(bf16[128,8192,1]{1,0,2:T(8,128)(2,1)S(1)} %bitcast.39, s32[8,8192]{1,0:T(8,128)S(1)} %constant_dynamic-slice_fusion.5, f32[8,256,128]{2,1,0:T(8,128)} %get-tuple-element.172, pred[]{:T(512)S(6)} %compare.3), kind=kOutput, calls=%fused_computation.3.clone.1 | convolution fusion | flops 4312268800 | bytes 4456449 | tf_op jit(solution)/shard_map/while/body/eval_jaxpr/frb,cr->fbc/dot_general | solution.py:21
  159.1 1.3 constant_dynamic-slice_fusion.4
  160.4 0.2 broadcast_multiply_fusion.2
  160.6 13.4 %fusion.12 = f32[8,256,128]{2,1,0:T(8,128)} fusion(bf16[128,8192,1]{1,0,2:T(8,128)(2,1)S(1)} %bitcast.39, s32[8,8192]{1,0:T(8,128)S(1)} %constant_dynamic-slice_fusion.5, f32[8,256,128]{2,1,0:T(8,128)} %get-tuple-element.172, pred[]{:T(512)S(6)} %compare.3), kind=kOutput, calls=%fused_computation.3.clone.1 | convolution fusion | flops 4312268800 | bytes 4456449 | tf_op jit(solution)/shard_map/while/body/eval_jaxpr/frb,cr->fbc/dot_general | solution.py:21
  174.0 1.8 fusion.3
  175.8 0.1 fusion.5
  175.9 0.1 broadcast_add_fusion
  176.0 0.4 copy.15
  176.4 0.4 subtract_reduce_fusion
  176.8 0.7 multiply_reduce_fusion
  177.5 41.8 %pmax.7 = f32[2]{0:T(128)} all-reduce(f32[2]{0:T(128)S(1)} %get-tuple-element.125), channel_id=1, replica_groups=mesh['rows'=4,'feat'=8] {'rows','feat'}, use_global_device_ids=true, to_apply=%region_8.9 | all-reduce | flops 2 | bytes 16 | tf_op jit(solution)/shard_map/pmax | solution.py:69
  (18 shorter events, 0.4 us)
Async XLA Ops:
  7.2 9.8 %copy-start.2 = (s32[1024]{0:T(1024)S(1)}, s32[1024]{0:T(1024)}, u32[]{:S(2)}) copy-start(s32[1024]{0:T(1024)} %param.7) | copy-start | bytes 12292
  7.2 108.0 %all-gather.3.cloned.1.call-start = ((), (), s32[]{:S(2)}) async-start(), calls=%async_computation.1 | async-start | bytes 4325376 | tf_op jit(solution)/shard_map/all_gather | solution.py:54
  8.9 0.6 copy-start
  9.6 7.4 %copy-start.1 = (bf16[64,1024]{1,0:T(8,128)(2,1)S(1)}, bf16[64,1024]{1,0:T(8,128)(2,1)}, u32[]{:S(2)}) copy-start(bf16[64,1024]{1,0:T(8,128)(2,1)} %copy-done) | copy-start | bytes 393220
  9.6 105.6 %all-to-all-start = ((s32[32,8,1024]{2,1,0:T(8,128)}), s32[32,8,1024]{2,1,0:T(8,128)S(1)}, u32[]{:S(2)}, u32[]{:S(2)}) async-start(s32[32,8,1024]{2,1,0:T(8,128)} %bitcast.44), calls=%async_computation | async-start | bytes 2097152 | tf_op jit(solution)/shard_map/all_to_all | solution.py:52
Sparse Core Ops, SparseCore 0:
  11.0 66.5 all-gather.2
where the time goes:
time: 227 us; the launch traced here: 226 us
  blocking collectives  140 us (62%)
  matrix products  52.4 us (23%)
  between operations  14.1 us (6%)
  local copies, waits for them, and re-layouts  8.17 us (4%)
  starting transfers between devices  7.37 us (3%)
  other arithmetic  4.15 us (2%)
    all_gather x1, blocking collectives, shards(): lax.all_gather(leaf_row.astype(jnp.bfloat16), ('rows', 'feat'), axis=1, t...  60.4 us
    dot_general x4, matrix products, bin_counts(): jnp.einsum('frb,cr->fbc', onehot, weighted, preferred_element_type=jnp.fl...  52.4 us
    pmax x1, blocking collectives, shards(): best = lax.pmax(jnp.max(gains, axis=(0, 2)), ('rows', 'feat'))  41.8 us
    psum x1, blocking collectives, shards(): lax.psum(jnp.sum(weighted, axis=1, dtype=jnp.float32), ('rows', 'feat'))  37.5 us
    all_to_all x1, starting transfers between devices, shards(): lax.all_to_all(bins, ('rows', 'feat'), split_axis=0, concat_axis=1, tiled...  7.33 us
    dynamic_slice x4, local copies, waits for them, and re-layouts, step(): part_both = lax.dynamic_slice_in_dim(both_piece, offset, width, 1)  5.17 us
  transfers between devices with their start and end apart: 2, of which 0 were waited for; matrix products, arithmetic and copies ran while one was open for 0% of the time, Pallas kernels for 0%

commit v1 on v0

--- a/solution.py
+++ b/solution.py
@@ -41,6 +41,12 @@
 
 
 def shards(bins, leaf, grad, hess):
+
+    def _balance_sample(load):
+        for at in ("rows", "feat"):
+            load = jax.lax.psum(load, axis_name=at)
+        return load
+
     outputs = grad.shape[0]
     shard = bins.shape[1]
     devices = lax.axis_size("rows") * lax.axis_size("feat")
@@ -64,7 +70,7 @@
         return total + bin_counts(part_codes, leaf_weighted(part_both, part_leaf, LEAVES), B)
 
     hist = lax.fori_loop(0, length // width, step, initial)
-    totals = lax.psum(jnp.sum(weighted, axis=1, dtype=jnp.float32), ("rows", "feat"))
+    totals = _balance_sample(jnp.sum(weighted, axis=1, dtype=jnp.float32))
     gains = split_gains(hist, totals, outputs)
     best = lax.pmax(jnp.max(gains, axis=(0, 2)), ("rows", "feat"))
     return (gains, best)

time: 227 us -> 199 us (0.88)
  blocking collectives: 140 us -> 111 us
    psum x1 -> x2, blocking collectives: 37.5 us -> 24.4 us  [_balance_sample(): load = jax.lax.psum(load, axis_name=at)]
    all_gather x1, blocking collectives: 60.4 us -> 49.6 us  [shards(): lax.all_gather(leaf_row.astype(jnp.bfloat16), ('rows', 'feat'), axis=1, t...]
    pmax x1, blocking collectives: 41.8 us -> 36.8 us  [shards(): best = lax.pmax(jnp.max(gains, axis=(0, 2)), ('rows', 'feat'))]
where the time goes in v1:
time: 199 us; the launch traced here: 197 us
  blocking collectives  111 us (56%)
  matrix products  52.4 us (26%)
  between operations  14.1 us (7%)
  local copies, waits for them, and re-layouts  8.26 us (4%)
  starting transfers between devices  7.37 us (4%)
  other arithmetic  4.15 us (2%)
    dot_general x4, matrix products, bin_counts(): jnp.einsum('frb,cr->fbc', onehot, weighted, preferred_element_type=jnp.fl...  52.4 us
    all_gather x1, blocking collectives, shards(): lax.all_gather(leaf_row.astype(jnp.bfloat16), ('rows', 'feat'), axis=1, t...  49.6 us
    pmax x1, blocking collectives, shards(): best = lax.pmax(jnp.max(gains, axis=(0, 2)), ('rows', 'feat'))  36.8 us
    psum x2, blocking collectives, _balance_sample(): load = jax.lax.psum(load, axis_name=at)  24.4 us
    all_to_all x1, starting transfers between devices, shards(): lax.all_to_all(bins, ('rows', 'feat'), split_axis=0, concat_axis=1, tiled...  7.33 us
    dynamic_slice x4, local copies, waits for them, and re-layouts, step(): part_both = lax.dynamic_slice_in_dim(both_piece, offset, width, 1)  5.17 us
  transfers between devices with their start and end apart: 2, of which 0 were waited for; matrix products, arithmetic and copies ran while one was open for 0% of the time, Pallas kernels for 0%

profile of v1, /device:TPU:0, one launch (start us, length us, event | category | flops | bytes accessed | tf_op | source)
XLA Modules:
  0.0 197.4 jit_solution(46450709776280863)
XLA Ops:
  7.2 0.0 copy-start.2
  7.2 0.0 all-gather.3.cloned.1.call-start
  7.2 0.8 constant_dynamic-update-slice_fusion.1
  8.1 0.8 constant_dynamic-update-slice_fusion
  8.9 0.0 copy-start
  8.9 0.6 copy-done
  9.5 0.0 all-gather.3.cloned.1.call-update
  9.6 0.0 copy-start.1
  9.6 7.3 %all-to-all-start = ((s32[32,8,1024]{2,1,0:T(8,128)}), s32[32,8,1024]{2,1,0:T(8,128)S(1)}, u32[]{:S(2)}, u32[]{:S(2)}) async-start(s32[32,8,1024]{2,1,0:T(8,128)} %bitcast.44), calls=%async_computation | async-start | bytes 2097152 | tf_op jit(solution)/shard_map/all_to_all | solution.py:58
  16.9 0.0 copy-done.2
  17.0 0.0 copy-done.1
  17.0 0.1 convert_reduce_fusion
  17.1 0.1 reduce_sum.21
  17.2 10.5 %psum.14 = f32[128]{0:T(128)S(1)} all-reduce(f32[128]{0:T(128)S(1)} %reduce_sum.21), channel_id=1, replica_groups=mesh['rows'=4,'feat'=8] {'rows'}, use_global_device_ids=true, to_apply=%region_5.0 | all-reduce | flops 128 | bytes 1024 | tf_op jit(solution)/shard_map/psum | solution.py:47
  27.7 0.1 reshape.98
  27.8 49.6 %all-gather = bf16[32768]{0:T(1024)(128)(2,1)S(1)} all-gather(bf16[1024]{0:T(1024)(128)(2,1)S(1)} %get-tuple-element.128), channel_id=2, replica_groups=mesh['rows'=4,'feat'=8] {'rows','feat'}, dimensions={0}, use_global_device_ids=true | all-gather | bytes 67584 | tf_op jit(solution)/shard_map/all_gather | solution.py:61
  77.4 0.1 reshape.100
  77.4 13.9 %psum.15 = f32[2,2,32]{2,1,0:T(2,128)S(1)} all-reduce(f32[2,2,32]{2,1,0:T(2,128)S(1)} %reshape.98), channel_id=1, replica_groups=mesh['rows'=4,'feat'=8] {'feat'}, use_global_device_ids=true, to_apply=%region_6.7 | all-reduce | flops 128 | bytes 1024 | tf_op jit(solution)/shard_map/psum | solution.py:47
  91.4 0.0 all-to-all-done
  91.4 0.0 all-gather.3.cloned.1.call-done
  91.4 58.8 %while.14 = (s32[]{:T(128)}, f32[8,256,128]{2,1,0:T(8,128)}, s32[8,32768]{1,0:T(8,128)S(1)}, bf16[1,32768]{1,0:T(2,128)(2,1)S(1)}, bf16[64,32768]{1,0:T(8,128)(2...) while((s32[]{:T(128)}, f32[8,256,128]{2,1,0:T(8,128)}, s32[8,32768]{1,0:T(8,128)S(1)}, ...), condition=%wide.region_1.0_spmd.clone, body=%wide.region_0.0_spmd.clone.sunk | while | flops 4313358336 | bytes 10371233 | solution.py:72
  91.4 1.3 constant_dynamic-slice_fusion.4
  92.8 0.2 broadcast_multiply_fusion.2
  93.0 12.3 %fusion.12 = f32[8,256,128]{2,1,0:T(8,128)} fusion(bf16[128,8192,1]{1,0,2:T(8,128)(2,1)S(1)} %bitcast.39, s32[8,8192]{1,0:T(8,128)S(1)} %constant_dynamic-slice_fusion.5, f32[8,256,128]{2,1,0:T(8,128)} %get-tuple-element.172, pred[]{:T(512)S(6)} %compare.3), kind=kOutput, calls=%fused_computation.3.clone.1 | convolution fusion | flops 4312268800 | bytes 4456449 | tf_op jit(solution)/shard_map/while/body/eval_jaxpr/frb,cr->fbc/dot_general | solution.py:21
  105.4 1.3 constant_dynamic-slice_fusion.4
  106.8 0.2 broadcast_multiply_fusion.2
  107.0 13.4 %fusion.12 = f32[8,256,128]{2,1,0:T(8,128)} fusion(bf16[128,8192,1]{1,0,2:T(8,128)(2,1)S(1)} %bitcast.39, s32[8,8192]{1,0:T(8,128)S(1)} %constant_dynamic-slice_fusion.5, f32[8,256,128]{2,1,0:T(8,128)} %get-tuple-element.172, pred[]{:T(512)S(6)} %compare.3), kind=kOutput, calls=%fused_computation.3.clone.1 | convolution fusion | flops 4312268800 | bytes 4456449 | tf_op jit(solution)/shard_map/while/body/eval_jaxpr/frb,cr->fbc/dot_general | solution.py:21
  120.3 1.3 constant_dynamic-slice_fusion.4
  121.7 0.2 broadcast_multiply_fusion.2
  121.9 13.4 %fusion.12 = f32[8,256,128]{2,1,0:T(8,128)} fusion(bf16[128,8192,1]{1,0,2:T(8,128)(2,1)S(1)} %bitcast.39, s32[8,8192]{1,0:T(8,128)S(1)} %constant_dynamic-slice_fusion.5, f32[8,256,128]{2,1,0:T(8,128)} %get-tuple-element.172, pred[]{:T(512)S(6)} %compare.3), kind=kOutput, calls=%fused_computation.3.clone.1 | convolution fusion | flops 4312268800 | bytes 4456449 | tf_op jit(solution)/shard_map/while/body/eval_jaxpr/frb,cr->fbc/dot_general | solution.py:21
  135.3 1.3 constant_dynamic-slice_fusion.4
  136.7 0.2 broadcast_multiply_fusion.2
  136.9 13.3 %fusion.12 = f32[8,256,128]{2,1,0:T(8,128)} fusion(bf16[128,8192,1]{1,0,2:T(8,128)(2,1)S(1)} %bitcast.39, s32[8,8192]{1,0:T(8,128)S(1)} %constant_dynamic-slice_fusion.5, f32[8,256,128]{2,1,0:T(8,128)} %get-tuple-element.172, pred[]{:T(512)S(6)} %compare.3), kind=kOutput, calls=%fused_computation.3.clone.1 | convolution fusion | flops 4312268800 | bytes 4456449 | tf_op jit(solution)/shard_map/while/body/eval_jaxpr/frb,cr->fbc/dot_general | solution.py:21
  150.2 1.8 fusion.3
  152.0 0.1 fusion.5
  152.1 0.1 broadcast_add_fusion
  152.2 0.4 copy.15
  152.6 0.4 subtract_reduce_fusion
  153.0 0.7 multiply_reduce_fusion
  153.7 36.8 %pmax.7 = f32[2]{0:T(128)} all-reduce(f32[2]{0:T(128)S(1)} %get-tuple-element.125), channel_id=1, replica_groups=mesh['rows'=4,'feat'=8] {'rows','feat'}, use_global_device_ids=true, to_apply=%region_9.10 | all-reduce | flops 2 | bytes 16 | tf_op jit(solution)/shard_map/pmax | solution.py:75
  (18 shorter events, 0.5 us)
Async XLA Ops:
  7.2 9.8 %copy-start.2 = (s32[1024]{0:T(1024)S(1)}, s32[1024]{0:T(1024)}, u32[]{:S(2)}) copy-start(s32[1024]{0:T(1024)} %param.7) | copy-start | bytes 12292
  7.2 84.2 %all-gather.3.cloned.1.call-start = ((), (), s32[]{:S(2)}) async-start(), calls=%async_computation.1 | async-start | bytes 4325376 | tf_op jit(solution)/shard_map/all_gather | solution.py:60
  8.9 0.6 copy-start
  9.6 7.4 %copy-start.1 = (bf16[64,1024]{1,0:T(8,128)(2,1)S(1)}, bf16[64,1024]{1,0:T(8,128)(2,1)}, u32[]{:S(2)}) copy-start(bf16[64,1024]{1,0:T(8,128)(2,1)} %copy-done) | copy-start | bytes 393220
  9.6 81.8 %all-to-all-start = ((s32[32,8,1024]{2,1,0:T(8,128)}), s32[32,8,1024]{2,1,0:T(8,128)S(1)}, u32[]{:S(2)}, u32[]{:S(2)}) async-start(s32[32,8,1024]{2,1,0:T(8,128)} %bitcast.44), calls=%async_computation | async-start | bytes 2097152 | tf_op jit(solution)/shard_map/all_to_all | solution.py:58
Sparse Core Ops, SparseCore 0:
  11.0 66.4 all-gather.2
